TPU v7x, 512 devices: a whole 4x4x16 slice. The times are simulated.
512 devices in a mesh: aper: 64 (over z_lo, y, x), rng: 4 (over z_hi), beam: 2 (over core).
Axes of the slice: x: 4, y: 4, z: 16 (z_hi: 4, z_lo: 4; z = z_hi * 4 + z_lo), core: 2. Of those that a mesh axis runs over, the one named last changes fastest.
Arguments:
- children: float32 [64, 2, 8192, 256], P('aper', None, 'rng', 'beam'), may hold values from -6 to 6
- shift_one: int32 [2, 256], replicated, may hold values from -8 to 8
- rtaps_one: float32 [2, 8, 256], replicated, may hold values from -2 to 2
- bstart_one: int32 [2, 512], replicated, may hold values from -5 to 252, as said below
- btaps_one: float32 [2, 8, 512], replicated, may hold values from -2 to 2
- prate_one: float32 [2, 512], replicated, may hold values from -64 to 64
- poff_one: float32 [2, 512], replicated, may hold values from -3.140625 to 3.140625
- shift_two: int32 [2, 512], replicated, may hold values from -8 to 8
- rtaps_two: float32 [2, 8, 512], replicated, may hold values from -2 to 2
- bstart_two: int32 [2, 1024], replicated, may hold values from -5 to 508, as said below
- btaps_two: float32 [2, 8, 1024], replicated, may hold values from -2 to 2
- prate_two: float32 [2, 1024], replicated, may hold values from -64 to 64
- poff_two: float32 [2, 1024], replicated, may hold values from -3.140625 to 3.140625
Outputs:
- merged: float32 [64, 2, 8192, 256], P('aper', None, 'rng', 'beam')
Inputs may be any that keep to these rules, and one draw needn't show every extreme that they name: bstart_one[c, b] is b // 2 - 8 // 2 plus -1, 0 or 1. bstart_two[c, b] is b // 2 - 8 // 2 plus -1, 0 or 1.
All inputs are finite; a program needn't handle non-finite values.
Results may differ from a plain program's by a relative error of at most 0.0003.
Values sent between devices are 32-bit elements; how exact they have to be, the bound alone decides.
A program may use at most 64 MiB of HBM per device.

v0:
```python
import functools

import jax
import jax.numpy as jnp
from jax import lax
from jax.experimental import pallas as pl
from jax.experimental.pallas import tpu as pltpu
from jax.sharding import PartitionSpec as P

MESH = pl.DeviceIdType.MESH
ROWS = 2048
BEAM = 128
CHUNK = 256
CHUNKS = ROWS // CHUNK
FIRST = 5
WIN = 48
TAPS = 8
OFFS = 24
RIM = 16
TOP = 32
SUB = 16
F32 = jnp.float32
BF16 = jnp.bfloat16


def split_bf16(x):
    hi = x.astype(BF16)
    lo = (x - hi.astype(F32)).astype(BF16)
    return hi, lo


def range_table(shift_row, tap_rows, out_ref):
    for o in range(OFFS):
        acc = jnp.zeros((1, BEAM), F32)
        for k in range(TAPS):
            acc = acc + jnp.where(shift_row + (8 + k) == o, tap_rows[k : k + 1], 0.0)
        out_ref[o] = jnp.broadcast_to(acc, (8, BEAM))


def beam_matrix(rows, start_row, tap_rows):
    ids = lax.broadcasted_iota(jnp.int32, (rows, BEAM), 0)
    acc = jnp.zeros((rows, BEAM), F32)
    for k in range(TAPS):
        acc = acc + jnp.where(ids == start_row + k, tap_rows[k : k + 1], 0.0)
    return acc


def phase_tables(rate, off, base, lead, near_c, near_s, far_c, far_s, tmp_c, tmp_s):
    scale = 1.0 / 8192.0
    r8 = lax.broadcasted_iota(jnp.int32, (8, BEAM), 0).astype(F32) * scale
    r32 = (lax.broadcasted_iota(jnp.int32, (32, BEAM), 0) * 8).astype(F32) * scale
    r16 = (base + lax.broadcasted_iota(jnp.int32, (16, BEAM), 0) * CHUNK - lead).astype(F32) * scale
    far = rate * r16 + off
    far_c[...] = jnp.cos(far)
    far_s[...] = jnp.sin(far)
    small = rate * r8
    sc, ss = jnp.cos(small), jnp.sin(small)
    big = rate * r32
    tmp_c[...] = jnp.cos(big)
    tmp_s[...] = jnp.sin(big)

    def fill(q, carry):
        bc = tmp_c[pl.ds(q, 1), :]
        bs = tmp_s[pl.ds(q, 1), :]
        at = pl.ds(pl.multiple_of(q * 8, 8), 8)
        near_c[at, :] = bc * sc - bs * ss
        near_s[at, :] = bs * sc + bc * ss
        return carry

    lax.fori_loop(0, 32, fill, 0)


def kernel(
    child_hbm,
    sh1,
    rt1,
    bs1,
    bt1,
    pr1,
    po1,
    sh2,
    rt2,
    bs2,
    bt2,
    pr2,
    po2,
    out,
    child,
    wide,
    turned,
    got,
    mixed,
    parent,
    packed,
    tab1,
    tab2,
    mat1,
    mat2a,
    mat2b,
    near_c,
    near_s,
    far_c,
    far_s,
    tmp_c,
    tmp_s,
    in_sem,
    zs_sem,
    zr_sem,
    ps_sem,
    pr_sem,
    es_sem,
    er_sem,
    xs_sem,
    xr_sem,
):
    aper = lax.axis_index("aper")
    rng = lax.axis_index("rng")
    beam = lax.axis_index("beam")
    me = lax.rem(aper, 4)
    group = aper - me
    block = 4 * beam + me
    up, down = lax.rem(rng + 3, 4), lax.rem(rng + 1, 4)

    def peer(d):
        return lax.rem(me + d, 4)

    def chunk_of(t):
        return lax.rem(t + FIRST, CHUNKS)

    load = pltpu.make_async_copy(child_hbm.at[0], child.at[:, pl.ds(RIM, ROWS), :], in_sem)
    load.start()

    barrier = pltpu.get_barrier_semaphore()
    for d in (1, 2, 3):
        pl.semaphore_signal(
            barrier, inc=1, device_id=(group + peer(d), rng, beam), device_id_type=MESH
        )
    pl.semaphore_signal(barrier, inc=1, device_id=(aper, rng, 1 - beam), device_id_type=MESH)
    pl.semaphore_signal(barrier, inc=1, device_id=(aper, up, beam), device_id_type=MESH)
    pl.semaphore_signal(barrier, inc=1, device_id=(aper, down, beam), device_id_type=MESH)

    @pl.when(beam == 0)
    def _():
        turned[:, 0:8, :] = jnp.zeros((2, 8, ROWS), F32)

    @pl.when(beam == 1)
    def _():
        turned[:, 136:144, :] = jnp.zeros((2, 8, ROWS), F32)

    side = lax.div(me, 2)
    own = pl.ds(pl.multiple_of(beam * BEAM, BEAM), BEAM)
    shift_row = jnp.where(side == 0, sh1[0:1, own], sh1[1:2, own])
    range_table(shift_row, rt1[side, :, own], tab1)

    pl.semaphore_wait(barrier, 6)
    load.wait()

    def halo(buf, sem_s, sem_r, first, last, low, high):
        return (
            pltpu.make_async_remote_copy(
                src_ref=buf.at[:, pl.ds(first, RIM), :],
                dst_ref=buf.at[:, pl.ds(high, RIM), :],
                send_sem=sem_s.at[0],
                recv_sem=sem_r.at[0],
                device_id=(aper, up, beam),
                device_id_type=MESH,
            ),
            pltpu.make_async_remote_copy(
                src_ref=buf.at[:, pl.ds(last, RIM), :],
                dst_ref=buf.at[:, pl.ds(low, RIM), :],
                send_sem=sem_s.at[1],
                recv_sem=sem_r.at[1],
                device_id=(aper, down, beam),
                device_id_type=MESH,
            ),
        )

    zc = halo(child, zs_sem, zr_sem, RIM, ROWS, 0, RIM + ROWS)
    zp = halo(parent, ps_sem, pr_sem, TOP, TOP + ROWS - RIM, TOP - RIM, TOP + ROWS)
    for c in zc:
        c.start()

    def edge_copy(t):
        at = pl.ds(pl.multiple_of(chunk_of(t) * CHUNK, CHUNK), CHUNK)
        return pltpu.make_async_remote_copy(
            src_ref=turned.at[:, pl.ds(pl.multiple_of(128 - 120 * beam, 8), 8), at],
            dst_ref=turned.at[:, pl.ds(pl.multiple_of(136 * beam, 8), 8), at],
            send_sem=es_sem.at[t],
            recv_sem=er_sem.at[t],
            device_id=(aper, rng, 1 - beam),
            device_id_type=MESH,
        )

    def window_copy(t, d):
        at = pl.ds(pl.multiple_of(chunk_of(t) * CHUNK, CHUNK), CHUNK)
        to = peer(d)
        return pltpu.make_async_remote_copy(
            src_ref=turned.at[:, pl.ds(pl.multiple_of(32 * to, 8), WIN), at],
            dst_ref=got.at[me, :, :, at],
            send_sem=xs_sem.at[d - 1, t],
            recv_sem=xr_sem.at[d - 1, t],
            device_id=(group + to, rng, beam),
            device_id_type=MESH,
        )

    def produce(t):
        j = chunk_of(t)
        base = pl.multiple_of(j * CHUNK, CHUNK)

        def rows(s, carry):
            first = base + s * 32
            for comp in range(2):
                acc = [jnp.zeros((8, BEAM), F32) for _ in range(4)]
                for o in range(OFFS):
                    w = tab1[o]
                    for v in range(4):
                        acc[v] = acc[v] + w * child[comp, pl.ds(first + (o + 4 + 8 * v), 8), :]
                for v in range(4):
                    wide[comp, pl.ds(pl.multiple_of(s * 32 + 8 * v, 8), 8), :] = acc[v]
            return carry

        lax.fori_loop(0, CHUNK // 32, rows, 0)
        for comp in range(2):
            for half in range(CHUNK // BEAM):
                turned[
                    comp, 8:136, pl.ds(pl.multiple_of(base + half * BEAM, BEAM), BEAM)
                ] = jnp.transpose(wide[comp, half * BEAM : (half + 1) * BEAM, :])

    def send(t):
        edge_copy(t).wait_recv()
        for d in (1, 3, 2):
            window_copy(t, d).start()
        at = pl.ds(pl.multiple_of(chunk_of(t) * CHUNK, CHUNK), CHUNK)
        got[me, :, :, at] = turned[:, pl.ds(pl.multiple_of(32 * me, 8), WIN), at]

    def produce_step(t, carry):
        @pl.when(t == 2)
        def _():
            for c in zc:
                c.wait_recv()

            @pl.when(rng == 0)
            def _():
                child[:, 0:RIM, :] = jnp.zeros((2, RIM, BEAM), F32)

            @pl.when(rng == 3)
            def _():
                child[:, RIM + ROWS :, :] = jnp.zeros((2, RIM, BEAM), F32)

        produce(t)
        edge_copy(t).start()

        @pl.when(t > 0)
        def _():
            send(t - 1)

        return carry

    lax.fori_loop(0, CHUNKS, produce_step, 0)
    send(CHUNKS - 1)

    shift = lax.rem(520 - 64 * block, 512)

    def lanes(v):
        return pltpu.roll(v, shift, 1)[:, :BEAM]

    ints = lanes(jnp.concatenate([bs1[...], sh2[...], bs1[...], sh2[...]], axis=0))
    floats = lanes(jnp.concatenate([pr1[...], po1[...], pr1[...], po1[...]], axis=0))
    beams_here = lax.broadcasted_iota(jnp.int32, (TAPS, BEAM), 1) + (64 * block - 8)
    inside = jnp.logical_and(beams_here >= 0, beams_here < 512)
    final = pl.ds(pl.multiple_of(block * BEAM, BEAM), BEAM)
    for s in range(2):
        taps = jnp.where(inside, lanes(bt1[s]), 0.0)
        m = beam_matrix(WIN, ints[s : s + 1] - (32 * block - 8), taps)
        hi, lo = split_bf16(m)
        mat1[s, 0:WIN, :] = hi
        mat1[s, WIN : 2 * WIN, :] = hi
        mat1[s, 2 * WIN : 3 * WIN, :] = lo
        range_table(ints[2 + s : 3 + s], lanes(rt2[s]), tab2.at[s])
        m = beam_matrix(BEAM, bs2[s : s + 1, final] - (64 * block - 8), bt2[s, :, final])
        hi, lo = split_bf16(m)
        mat2a[s, 0:BEAM, :] = hi
        mat2a[s, BEAM : 2 * BEAM, :] = hi
        mat2b[s] = lo
        phase_tables(
            floats[s : s + 1],
            floats[2 + s : 3 + s],
            rng * ROWS,
            0,
            near_c.at[s],
            near_s.at[s],
            far_c.at[s],
            far_s.at[s],
            tmp_c,
            tmp_s,
        )
        phase_tables(
            pr2[s : s + 1, final],
            po2[s : s + 1, final],
            rng * ROWS,
            RIM,
            near_c.at[2 + s],
            near_s.at[2 + s],
            far_c.at[2 + s],
            far_s.at[2 + s],
            tmp_c,
            tmp_s,
        )

    def turn(level, j, rho):
        both = []
        for s in range(2):
            fc = far_c[2 * level + s, pl.ds(j, 1), :]
            fs = far_s[2 * level + s, pl.ds(j, 1), :]
            nc = near_c[2 * level + s, pl.ds(rho, SUB), :]
            ns = near_s[2 * level + s, pl.ds(rho, SUB), :]
            both.append((fc * nc - fs * ns, fs * nc + fc * ns))
        return both

    def make_parents(j):
        at = pl.ds(pl.multiple_of(j * CHUNK, CHUNK), CHUNK)
        for c in range(4):
            for comp in range(2):
                hi, lo = split_bf16(got[c, comp, :, at])
                mixed[2 * c + comp] = lax.dot_general(
                    jnp.concatenate([hi, lo, hi], axis=0),
                    mat1[c // 2],
                    (((0,), (0,)), ((), ())),
                    preferred_element_type=F32,
                )

        def rows(s, carry):
            rho = pl.multiple_of(s * SUB, SUB)
            (c0, s0), (c1, s1) = turn(0, j, rho)
            here = pl.ds(rho, SUB)
            to = pl.ds(pl.multiple_of(TOP + j * CHUNK + rho, SUB), SUB)
            for e in range(2):
                lr, li = mixed[2 * e, here, :], mixed[2 * e + 1, here, :]
                rr, ri = mixed[4 + 2 * e, here, :], mixed[5 + 2 * e, here, :]
                parent[2 * e, to, :] = (c0 * lr - s0 * li) + (c1 * rr - s1 * ri)
                parent[2 * e + 1, to, :] = (s0 * lr + c0 * li) + (s1 * rr + c1 * ri)
            return carry

        lax.fori_loop(0, CHUNK // SUB, rows, 0)

    def range_two(first, slot):
        for e in range(2):
            acc = [[jnp.zeros((8, BEAM), F32) for _ in range(2)] for _ in range(2)]
            for o in range(OFFS):
                w = tab2[e, o]
                for comp in range(2):
                    for v in range(2):
                        acc[comp][v] = acc[comp][v] + w * parent[
                            2 * e + comp, pl.ds(first + (TOP - 12 + o + 8 * v), 8), :
                        ]
            for comp in range(2):
                hi, lo = split_bf16(jnp.concatenate(acc[comp], axis=0))
                packed[2 * e + comp, pl.ds(slot, SUB), 0:BEAM] = hi
                packed[2 * e + comp, pl.ds(slot, SUB), BEAM : 2 * BEAM] = lo

    def products(count):
        for e in range(2):
            for comp in range(2):
                z = packed[2 * e + comp, 0:count, :]
                mixed[2 * e + comp, 0:count, :] = jnp.dot(
                    z, mat2a[e], preferred_element_type=F32
                ) + jnp.dot(z[:, :BEAM], mat2b[e], preferred_element_type=F32)

    def finish(first, slot, j, rho):
        (c0, s0), (c1, s1) = turn(1, j, rho)
        here = pl.ds(slot, SUB)
        to = pl.ds(first, SUB)
        lr, li, rr, ri = (mixed[i, here, :] for i in range(4))
        out[0, 0, to, :] = (c0 * lr - s0 * li) + (c1 * rr - s1 * ri)
        out[0, 1, to, :] = (s0 * lr + c0 * li) + (s1 * rr + c1 * ri)

    def consume_step(t, carry):
        j = chunk_of(t)
        for d in (1, 3, 2):
            window_copy(t, d).wait_recv()
        make_parents(j)

        @pl.when(j == 0)
        def _():
            for c in zp:
                c.start()

        begin = jnp.where(jnp.logical_or(t == 0, j == 0), 2, 0)

        def rows_in(s, carry):
            slot = pl.multiple_of(s * SUB, SUB)
            range_two(pl.multiple_of(j * CHUNK - RIM + slot, SUB), slot)
            return carry

        def rows_out(s, carry):
            slot = pl.multiple_of(s * SUB, SUB)
            finish(pl.multiple_of(j * CHUNK - RIM + slot, SUB), slot, j, slot)
            return carry

        lax.fori_loop(begin, CHUNK // SUB, rows_in, 0)
        products(CHUNK)
        lax.fori_loop(begin, CHUNK // SUB, rows_out, 0)
        return carry

    lax.fori_loop(0, CHUNKS, consume_step, 0)

    for c in zp:
        c.wait_recv()

    @pl.when(rng == 0)
    def _():
        parent[:, TOP - RIM : TOP, :] = jnp.zeros((4, RIM, BEAM), F32)

    @pl.when(rng == 3)
    def _():
        parent[:, TOP + ROWS : TOP + ROWS + RIM, :] = jnp.zeros((4, RIM, BEAM), F32)

    joint = FIRST * CHUNK
    strips = (
        (0, 0, RIM),
        (joint - RIM, FIRST, 0),
        (joint, FIRST, RIM),
        (ROWS - RIM, CHUNKS, 0),
    )
    for n, (first, j, rho) in enumerate(strips):
        range_two(first, n * SUB)
    products(len(strips) * SUB)
    for n, (first, j, rho) in enumerate(strips):
        finish(first, n * SUB, j, rho)

    for c in zc + zp:
        c.wait_send()

    def drain(t, carry):
        edge_copy(t).wait_send()
        for d in (1, 3, 2):
            window_copy(t, d).wait_send()
        return carry

    lax.fori_loop(0, CHUNKS, drain, 0)


def body(*args):
    vmem = pl.BlockSpec(memory_space=pltpu.VMEM)
    dma = pltpu.SemaphoreType.DMA
    return pl.pallas_call(
        kernel,
        out_shape=jax.ShapeDtypeStruct((1, 2, ROWS, BEAM), F32),
        in_specs=[pl.BlockSpec(memory_space=pl.ANY)] + [vmem] * 12,
        out_specs=vmem,
        scratch_shapes=[
            pltpu.VMEM((2, ROWS + 2 * RIM, BEAM), F32),
            pltpu.VMEM((2, CHUNK, BEAM), F32),
            pltpu.VMEM((2, BEAM + 16, ROWS), F32),
            pltpu.VMEM((4, 2, WIN, ROWS), F32),
            pltpu.VMEM((8, CHUNK, BEAM), F32),
            pltpu.VMEM((4, TOP + ROWS + 32, BEAM), F32),
            pltpu.VMEM((4, CHUNK, 2 * BEAM), BF16),
            pltpu.VMEM((OFFS, 8, BEAM), F32),
            pltpu.VMEM((2, OFFS, 8, BEAM), F32),
            pltpu.VMEM((2, 3 * WIN, BEAM), BF16),
            pltpu.VMEM((2, 2 * BEAM, BEAM), BF16),
            pltpu.VMEM((2, BEAM, BEAM), BF16),
            pltpu.VMEM((4, CHUNK, BEAM), F32),
            pltpu.VMEM((4, CHUNK, BEAM), F32),
            pltpu.VMEM((4, 16, BEAM), F32),
            pltpu.VMEM((4, 16, BEAM), F32),
            pltpu.VMEM((32, BEAM), F32),
            pltpu.VMEM((32, BEAM), F32),
            dma,
            dma((2,)),
            dma((2,)),
            dma((2,)),
            dma((2,)),
            dma((CHUNKS,)),
            dma((CHUNKS,)),
            dma((3, CHUNKS)),
            dma((3, CHUNKS)),
        ],
        compiler_params=pltpu.CompilerParams(
            collective_id=0, has_side_effects=True, vmem_limit_bytes=40 * 2**20
        ),
        name="merge",
    )(*args)


def solution(mesh):
    return jax.shard_map(
        body,
        mesh=mesh,
        in_specs=(P("aper", None, "rng", "beam"),) + (P(),) * 12,
        out_specs=P("aper", None, "rng", "beam"),
        check_vma=False,
    )
```

profile of v0, /device:TPU:1, one launch (start us, length us, event | category | flops | bytes accessed | tf_op | source)
XLA Modules:
  0.0 66.9 jit_solution(10772389504721433845)
XLA Ops:
  0.0 0.0 copy-start
  0.0 1.6 %copy-done = f32[1,2,2048,128]{3,2,1,0:T(8,128)S(1)} copy-done((f32[1,2,2048,128]{3,2,1,0:T(8,128)S(1)}, f32[1,2,2048,128]{3,2,1,0:T(8,128)}, u32[]{:S(2)}) %copy-start) | copy-done | bytes 2097176
  1.6 0.0 copy-start.1
  1.6 0.8 %copy-done.1 = f32[2,8,1024]{2,1,0:T(8,128)S(1)} copy-done((f32[2,8,1024]{2,1,0:T(8,128)S(1)}, f32[2,8,1024]{2,1,0:T(8,128)}, u32[]{:S(2)}) %copy-start.1) | copy-done | bytes 65560
  2.4 0.0 copy-start.2
  2.4 0.8 %copy-done.2 = f32[2,8,512]{2,1,0:T(8,128)S(1)} copy-done((f32[2,8,512]{2,1,0:T(8,128)S(1)}, f32[2,8,512]{2,1,0:T(8,128)}, u32[]{:S(2)}) %copy-start.2) | copy-done | bytes 32792
  3.2 0.0 copy-start.3
  3.2 0.8 %copy-done.3 = f32[2,8,512]{2,1,0:T(8,128)S(1)} copy-done((f32[2,8,512]{2,1,0:T(8,128)S(1)}, f32[2,8,512]{2,1,0:T(8,128)}, u32[]{:S(2)}) %copy-start.3) | copy-done | bytes 32792
  3.9 0.0 copy-start.4
  4.0 0.7 %copy-done.4 = f32[2,8,256]{2,1,0:T(8,128)S(1)} copy-done((f32[2,8,256]{2,1,0:T(8,128)S(1)}, f32[2,8,256]{2,1,0:T(8,128)}, u32[]{:S(2)}) %copy-start.4) | copy-done | bytes 16408
  4.7 0.0 copy-start.5
  4.7 0.7 %copy-done.5 = s32[2,1024]{1,0:T(2,128)S(1)} copy-done((s32[2,1024]{1,0:T(2,128)S(1)}, s32[2,1024]{1,0:T(2,128)}, u32[]{:S(2)}) %copy-start.5) | copy-done | bytes 8216
  5.4 0.0 copy-start.6
  5.4 0.7 %copy-done.6 = f32[2,1024]{1,0:T(2,128)S(1)} copy-done((f32[2,1024]{1,0:T(2,128)S(1)}, f32[2,1024]{1,0:T(2,128)}, u32[]{:S(2)}) %copy-start.6) | copy-done | bytes 8216
  6.1 0.0 copy-start.7
  6.1 0.7 %copy-done.7 = f32[2,1024]{1,0:T(2,128)S(1)} copy-done((f32[2,1024]{1,0:T(2,128)S(1)}, f32[2,1024]{1,0:T(2,128)}, u32[]{:S(2)}) %copy-start.7) | copy-done | bytes 8216
  6.8 0.0 copy-start.8
  6.8 0.7 %copy-done.8 = s32[2,512]{1,0:T(2,128)S(1)} copy-done((s32[2,512]{1,0:T(2,128)S(1)}, s32[2,512]{1,0:T(2,128)}, u32[]{:S(2)}) %copy-start.8) | copy-done | bytes 4120
  7.4 0.0 copy-start.9
  7.4 0.7 %copy-done.9 = f32[2,512]{1,0:T(2,128)S(1)} copy-done((f32[2,512]{1,0:T(2,128)S(1)}, f32[2,512]{1,0:T(2,128)}, u32[]{:S(2)}) %copy-start.9) | copy-done | bytes 4120
  8.1 0.0 copy-start.10
  8.1 0.7 %copy-done.10 = f32[2,512]{1,0:T(2,128)S(1)} copy-done((f32[2,512]{1,0:T(2,128)S(1)}, f32[2,512]{1,0:T(2,128)}, u32[]{:S(2)}) %copy-start.10) | copy-done | bytes 4120
  8.8 0.0 copy-start.11
  8.8 0.7 %copy-done.11 = s32[2,512]{1,0:T(2,128)S(1)} copy-done((s32[2,512]{1,0:T(2,128)S(1)}, s32[2,512]{1,0:T(2,128)}, u32[]{:S(2)}) %copy-start.11) | copy-done | bytes 4120
  9.5 0.0 copy-start.12
  9.5 0.7 %copy-done.12 = s32[2,256]{1,0:T(2,128)S(1)} copy-done((s32[2,256]{1,0:T(2,128)S(1)}, s32[2,256]{1,0:T(2,128)}, u32[]{:S(2)}) %copy-start.12) | copy-done | bytes 2072
  10.2 55.3 %merge.1 = f32[1,2,2048,128]{3,2,1,0:T(8,128)S(1)} custom-call(f32[1,2,2048,128]{3,2,1,0:T(8,128)S(1)} %copy-done, s32[2,256]{1,0:T(2,128)S(1)} %copy-done.12, f32[2,8,256]{2,1,0:T(8,128)S(1)} %copy-done.4, s32[2,512]{1,0:T(2,128)S(1)} %copy-done.8, f32[2,8,512]{2,1,0:T(8,128)S(1)} %copy-done.2, f32[2,512]{1,0:T(2,128)S(1)} %copy-done.9, ...), custom_call_target="tpu_custom_call" | custom-call | tf_op jit(solution)/shard_map/merge/pallas_call | solution.py:446
  65.5 1.3 %copy.15 = f32[1,2,2048,128]{3,2,1,0:T(8,128)} copy(f32[1,2,2048,128]{3,2,1,0:T(8,128)S(1)} %merge.1) | data formatting | bytes 4194304
Async XLA Ops:
  0.0 1.6 %copy-start = (f32[1,2,2048,128]{3,2,1,0:T(8,128)S(1)}, f32[1,2,2048,128]{3,2,1,0:T(8,128)}, u32[]{:S(2)}) copy-start(f32[1,2,2048,128]{3,2,1,0:T(8,128)} %child_hbm.1) | copy-start | bytes 6291460
  1.6 0.8 %copy-start.1 = (f32[2,8,1024]{2,1,0:T(8,128)S(1)}, f32[2,8,1024]{2,1,0:T(8,128)}, u32[]{:S(2)}) copy-start(f32[2,8,1024]{2,1,0:T(8,128)} %bt2.1) | copy-start | bytes 196612
  2.4 0.8 %copy-start.2 = (f32[2,8,512]{2,1,0:T(8,128)S(1)}, f32[2,8,512]{2,1,0:T(8,128)}, u32[]{:S(2)}) copy-start(f32[2,8,512]{2,1,0:T(8,128)} %bt1.1) | copy-start | bytes 98308
  3.2 0.8 %copy-start.3 = (f32[2,8,512]{2,1,0:T(8,128)S(1)}, f32[2,8,512]{2,1,0:T(8,128)}, u32[]{:S(2)}) copy-start(f32[2,8,512]{2,1,0:T(8,128)} %rt2.1) | copy-start | bytes 98308
  3.9 0.7 %copy-start.4 = (f32[2,8,256]{2,1,0:T(8,128)S(1)}, f32[2,8,256]{2,1,0:T(8,128)}, u32[]{:S(2)}) copy-start(f32[2,8,256]{2,1,0:T(8,128)} %rt1.1) | copy-start | bytes 49156
  4.7 0.7 %copy-start.5 = (s32[2,1024]{1,0:T(2,128)S(1)}, s32[2,1024]{1,0:T(2,128)}, u32[]{:S(2)}) copy-start(s32[2,1024]{1,0:T(2,128)} %bs2.1) | copy-start | bytes 24580
  5.4 0.7 %copy-start.6 = (f32[2,1024]{1,0:T(2,128)S(1)}, f32[2,1024]{1,0:T(2,128)}, u32[]{:S(2)}) copy-start(f32[2,1024]{1,0:T(2,128)} %pr2.1) | copy-start | bytes 24580
  6.1 0.7 %copy-start.7 = (f32[2,1024]{1,0:T(2,128)S(1)}, f32[2,1024]{1,0:T(2,128)}, u32[]{:S(2)}) copy-start(f32[2,1024]{1,0:T(2,128)} %po2.1) | copy-start | bytes 24580
  6.8 0.7 %copy-start.8 = (s32[2,512]{1,0:T(2,128)S(1)}, s32[2,512]{1,0:T(2,128)}, u32[]{:S(2)}) copy-start(s32[2,512]{1,0:T(2,128)} %bs1.1) | copy-start | bytes 12292
  7.4 0.7 %copy-start.9 = (f32[2,512]{1,0:T(2,128)S(1)}, f32[2,512]{1,0:T(2,128)}, u32[]{:S(2)}) copy-start(f32[2,512]{1,0:T(2,128)} %pr1.1) | copy-start | bytes 12292
  8.1 0.7 %copy-start.10 = (f32[2,512]{1,0:T(2,128)S(1)}, f32[2,512]{1,0:T(2,128)}, u32[]{:S(2)}) copy-start(f32[2,512]{1,0:T(2,128)} %po1.1) | copy-start | bytes 12292
  8.8 0.7 %copy-start.11 = (s32[2,512]{1,0:T(2,128)S(1)}, s32[2,512]{1,0:T(2,128)}, u32[]{:S(2)}) copy-start(s32[2,512]{1,0:T(2,128)} %sh2.1) | copy-start | bytes 12292
  9.5 0.7 %copy-start.12 = (s32[2,256]{1,0:T(2,128)S(1)}, s32[2,256]{1,0:T(2,128)}, u32[]{:S(2)}) copy-start(s32[2,256]{1,0:T(2,128)} %sh1.1) | copy-start | bytes 6148
where the time goes:
time: 67.5 us; the launch traced here: 66.9 us
  Pallas kernels  55.3 us (82%)
  local copies, waits for them, and re-layouts  11.5 us (17%)
    pallas_call x1, Pallas kernels, body(): pl.pallas_call(kernel, out_shape=jax.ShapeDtypeStruct((1, 2, ROWS, BEAM),...  55.3 us
    unnamed x27, local copies, waits for them, and re-layouts  11.5 us

commit v1 on v0

--- a/solution.py
+++ b/solution.py
@@ -10,9 +10,13 @@
 MESH = pl.DeviceIdType.MESH
 ROWS = 2048
 BEAM = 128
-CHUNK = 256
+CHUNK = 128
 CHUNKS = ROWS // CHUNK
-FIRST = 5
+FIRST = 7
+EARLY = 3
+LEAD = 6
+NEAR = CHUNK + 32
+FAR = 24
 WIN = 48
 TAPS = 8
 OFFS = 24
@@ -48,14 +52,14 @@
 def phase_tables(rate, off, base, lead, near_c, near_s, far_c, far_s, tmp_c, tmp_s):
     scale = 1.0 / 8192.0
     r8 = lax.broadcasted_iota(jnp.int32, (8, BEAM), 0).astype(F32) * scale
-    r32 = (lax.broadcasted_iota(jnp.int32, (32, BEAM), 0) * 8).astype(F32) * scale
-    r16 = (base + lax.broadcasted_iota(jnp.int32, (16, BEAM), 0) * CHUNK - lead).astype(F32) * scale
-    far = rate * r16 + off
+    r24 = (lax.broadcasted_iota(jnp.int32, (24, BEAM), 0) * 8).astype(F32) * scale
+    rows = base + lax.broadcasted_iota(jnp.int32, (FAR, BEAM), 0) * CHUNK - lead
+    far = rate * (rows.astype(F32) * scale) + off
     far_c[...] = jnp.cos(far)
     far_s[...] = jnp.sin(far)
     small = rate * r8
     sc, ss = jnp.cos(small), jnp.sin(small)
-    big = rate * r32
+    big = rate * r24
     tmp_c[...] = jnp.cos(big)
     tmp_s[...] = jnp.sin(big)
 
@@ -67,11 +71,24 @@
         near_s[at, :] = bs * sc + bc * ss
         return carry
 
-    lax.fori_loop(0, 32, fill, 0)
+    lax.fori_loop(0, NEAR // 8, fill, 0)
 
 
 def kernel(
     child_hbm,
+    sh1_hbm,
+    rt1_hbm,
+    bs1_hbm,
+    bt1_hbm,
+    pr1_hbm,
+    po1_hbm,
+    sh2_hbm,
+    rt2_hbm,
+    bs2_hbm,
+    bt2_hbm,
+    pr2_hbm,
+    po2_hbm,
+    out,
     sh1,
     rt1,
     bs1,
@@ -84,7 +101,6 @@
     bt2,
     pr2,
     po2,
-    out,
     child,
     wide,
     turned,
@@ -92,6 +108,7 @@
     mixed,
     parent,
     packed,
+    image,
     tab1,
     tab2,
     mat1,
@@ -104,6 +121,10 @@
     tmp_c,
     tmp_s,
     in_sem,
+    out_sem,
+    tab_sem,
+    chip_sem,
+    core_sem,
     zs_sem,
     zr_sem,
     ps_sem,
@@ -128,32 +149,59 @@
         return lax.rem(t + FIRST, CHUNKS)
 
     load = pltpu.make_async_copy(child_hbm.at[0], child.at[:, pl.ds(RIM, ROWS), :], in_sem)
+    tables = [
+        pltpu.make_async_copy(src, dst, tab_sem.at[n])
+        for n, (src, dst) in enumerate(
+            (
+                (sh1_hbm, sh1),
+                (rt1_hbm, rt1),
+                (bs1_hbm, bs1),
+                (bt1_hbm, bt1),
+                (pr1_hbm, pr1),
+                (po1_hbm, po1),
+                (sh2_hbm, sh2),
+                (rt2_hbm, rt2),
+                (bs2_hbm, bs2),
+                (bt2_hbm, bt2),
+                (pr2_hbm, pr2),
+                (po2_hbm, po2),
+            )
+        )
+    ]
+    for c in tables[:2]:
+        c.start()
     load.start()
+    for c in tables[2:]:
+        c.start()
 
     barrier = pltpu.get_barrier_semaphore()
-    for d in (1, 2, 3):
-        pl.semaphore_signal(
-            barrier, inc=1, device_id=(group + peer(d), rng, beam), device_id_type=MESH
-        )
-    pl.semaphore_signal(barrier, inc=1, device_id=(aper, rng, 1 - beam), device_id_type=MESH)
-    pl.semaphore_signal(barrier, inc=1, device_id=(aper, up, beam), device_id_type=MESH)
-    pl.semaphore_signal(barrier, inc=1, device_id=(aper, down, beam), device_id_type=MESH)
+    partner = (aper, rng, 1 - beam)
 
     @pl.when(beam == 0)
     def _():
+        for d in (1, 2, 3):
+            pl.semaphore_signal(
+                barrier, inc=1, device_id=(group + peer(d), rng, beam), device_id_type=MESH
+            )
+
+    @pl.when(beam == 1)
+    def _():
+        pl.semaphore_signal(barrier, inc=1, device_id=partner, device_id_type=MESH)
+
+    @pl.when(beam == 0)
+    def _():
         turned[:, 0:8, :] = jnp.zeros((2, 8, ROWS), F32)
 
     @pl.when(beam == 1)
     def _():
         turned[:, 136:144, :] = jnp.zeros((2, 8, ROWS), F32)
 
+    for c in tables[:2]:
+        c.wait()
     side = lax.div(me, 2)
     own = pl.ds(pl.multiple_of(beam * BEAM, BEAM), BEAM)
     shift_row = jnp.where(side == 0, sh1[0:1, own], sh1[1:2, own])
     range_table(shift_row, rt1[side, :, own], tab1)
-
-    pl.semaphore_wait(barrier, 6)
-    load.wait()
 
     def halo(buf, sem_s, sem_r, first, last, low, high):
         return (
@@ -177,8 +225,6 @@
 
     zc = halo(child, zs_sem, zr_sem, RIM, ROWS, 0, RIM + ROWS)
     zp = halo(parent, ps_sem, pr_sem, TOP, TOP + ROWS - RIM, TOP - RIM, TOP + ROWS)
-    for c in zc:
-        c.start()
 
     def edge_copy(t):
         at = pl.ds(pl.multiple_of(chunk_of(t) * CHUNK, CHUNK), CHUNK)
@@ -233,32 +279,39 @@
         at = pl.ds(pl.multiple_of(chunk_of(t) * CHUNK, CHUNK), CHUNK)
         got[me, :, :, at] = turned[:, pl.ds(pl.multiple_of(32 * me, 8), WIN), at]
 
-    def produce_step(t, carry):
-        @pl.when(t == 2)
-        def _():
-            for c in zc:
-                c.wait_recv()
-
-            @pl.when(rng == 0)
-            def _():
-                child[:, 0:RIM, :] = jnp.zeros((2, RIM, BEAM), F32)
-
-            @pl.when(rng == 3)
-            def _():
-                child[:, RIM + ROWS :, :] = jnp.zeros((2, RIM, BEAM), F32)
-
+    load.wait()
+    for t in range(EARLY):
+        produce(t)
+
+    @pl.when(beam == 0)
+    def _():
+        pl.semaphore_wait(barrier, 4)
+        for d in (1, 2, 3):
+            pl.semaphore_signal(
+                chip_sem, inc=1, device_id=(group + peer(d), rng, beam), device_id_type=MESH
+            )
+        pl.semaphore_wait(chip_sem, 3)
+        pl.semaphore_signal(core_sem, inc=1, device_id=partner, device_id_type=MESH)
+
+    @pl.when(beam == 1)
+    def _():
+        pl.semaphore_wait(core_sem, 1)
+        for z in (up, down):
+            pl.semaphore_signal(barrier, inc=1, device_id=(aper, z, beam), device_id_type=MESH)
+
+    for t in range(EARLY):
+        edge_copy(t).start()
+    for t in range(EARLY, LEAD):
         produce(t)
         edge_copy(t).start()
-
-        @pl.when(t > 0)
-        def _():
+        if t == EARLY:
+            for before in range(EARLY):
+                send(before)
+        else:
             send(t - 1)
 
-        return carry
-
-    lax.fori_loop(0, CHUNKS, produce_step, 0)
-    send(CHUNKS - 1)
-
+    for c in tables[2:]:
+        c.wait()
     shift = lax.rem(520 - 64 * block, 512)
 
     def lanes(v):
@@ -307,6 +360,18 @@
             tmp_s,
         )
 
+    @pl.when(beam == 1)
+    def _():
+        pl.semaphore_wait(barrier, 2)
+        pl.semaphore_signal(core_sem, inc=1, device_id=partner, device_id_type=MESH)
+
+    @pl.when(beam == 0)
+    def _():
+        pl.semaphore_wait(core_sem, 1)
+
+    for c in zc:
+        c.start()
+
     def turn(level, j, rho):
         both = []
         for s in range(2):
@@ -322,7 +387,7 @@
         for c in range(4):
             for comp in range(2):
                 hi, lo = split_bf16(got[c, comp, :, at])
-                mixed[2 * c + comp] = lax.dot_general(
+                mixed[2 * c + comp, 0:CHUNK, :] = lax.dot_general(
                     jnp.concatenate([hi, lo, hi], axis=0),
                     mat1[c // 2],
                     (((0,), (0,)), ((), ())),
@@ -343,20 +408,21 @@
 
         lax.fori_loop(0, CHUNK // SUB, rows, 0)
 
-    def range_two(first, slot):
-        for e in range(2):
-            acc = [[jnp.zeros((8, BEAM), F32) for _ in range(2)] for _ in range(2)]
-            for o in range(OFFS):
-                w = tab2[e, o]
-                for comp in range(2):
-                    for v in range(2):
-                        acc[comp][v] = acc[comp][v] + w * parent[
-                            2 * e + comp, pl.ds(first + (TOP - 12 + o + 8 * v), 8), :
-                        ]
+    def range_two(first, slot, e, weights):
+        acc = [[jnp.zeros((8, BEAM), F32) for _ in range(2)] for _ in range(2)]
+        for o in range(OFFS):
             for comp in range(2):
-                hi, lo = split_bf16(jnp.concatenate(acc[comp], axis=0))
-                packed[2 * e + comp, pl.ds(slot, SUB), 0:BEAM] = hi
-                packed[2 * e + comp, pl.ds(slot, SUB), BEAM : 2 * BEAM] = lo
+                for v in range(2):
+                    acc[comp][v] = acc[comp][v] + weights[o] * parent[
+                        2 * e + comp, pl.ds(first + (TOP - 12 + o + 8 * v), 8), :
+                    ]
+        for comp in range(2):
+            hi, lo = split_bf16(jnp.concatenate(acc[comp], axis=0))
+            packed[2 * e + comp, pl.ds(slot, SUB), 0:BEAM] = hi
+            packed[2 * e + comp, pl.ds(slot, SUB), BEAM : 2 * BEAM] = lo
+
+    def range_weights(e):
+        return [tab2[e, o] for o in range(OFFS)]
 
     def products(count):
         for e in range(2):
@@ -371,25 +437,22 @@
         here = pl.ds(slot, SUB)
         to = pl.ds(first, SUB)
         lr, li, rr, ri = (mixed[i, here, :] for i in range(4))
-        out[0, 0, to, :] = (c0 * lr - s0 * li) + (c1 * rr - s1 * ri)
-        out[0, 1, to, :] = (s0 * lr + c0 * li) + (s1 * rr + c1 * ri)
-
-    def consume_step(t, carry):
+        image[0, to, :] = (c0 * lr - s0 * li) + (c1 * rr - s1 * ri)
+        image[1, to, :] = (s0 * lr + c0 * li) + (s1 * rr + c1 * ri)
+
+    def put(j):
+        at = pl.ds(pl.multiple_of(j * CHUNK, CHUNK), CHUNK)
+        return pltpu.make_async_copy(image.at[:, at, :], out.at[0, :, at, :], out_sem.at[j])
+
+    def consume(t, begin, end):
         j = chunk_of(t)
         for d in (1, 3, 2):
             window_copy(t, d).wait_recv()
         make_parents(j)
 
-        @pl.when(j == 0)
-        def _():
-            for c in zp:
-                c.start()
-
-        begin = jnp.where(jnp.logical_or(t == 0, j == 0), 2, 0)
-
-        def rows_in(s, carry):
+        def rows_in(s, carry, e, weights):
             slot = pl.multiple_of(s * SUB, SUB)
-            range_two(pl.multiple_of(j * CHUNK - RIM + slot, SUB), slot)
+            range_two(pl.multiple_of(j * CHUNK - RIM + slot, SUB), slot, e, weights)
             return carry
 
         def rows_out(s, carry):
@@ -397,12 +460,62 @@
             finish(pl.multiple_of(j * CHUNK - RIM + slot, SUB), slot, j, slot)
             return carry
 
-        lax.fori_loop(begin, CHUNK // SUB, rows_in, 0)
-        products(CHUNK)
-        lax.fori_loop(begin, CHUNK // SUB, rows_out, 0)
+        for e in range(2):
+            lax.fori_loop(
+                begin, end, functools.partial(rows_in, e=e, weights=range_weights(e)), 0
+            )
+        products(end * SUB)
+        lax.fori_loop(begin, end, rows_out, 0)
+
+    def step(t, carry):
+        j = chunk_of(t)
+
+        @pl.when(t + LEAD - 1 < CHUNKS)
+        def _():
+            send(t + LEAD - 1)
+
+        @pl.when(t + LEAD < CHUNKS)
+        def _():
+            @pl.when(t + LEAD == CHUNKS - 1 - FIRST)
+            def _():
+                for c in zc:
+                    c.wait_recv()
+
+                @pl.when(rng == 0)
+                def _():
+                    child[:, 0:RIM, :] = jnp.zeros((2, RIM, BEAM), F32)
+
+                @pl.when(rng == 3)
+                def _():
+                    child[:, RIM + ROWS :, :] = jnp.zeros((2, RIM, BEAM), F32)
+
+            produce(t + LEAD)
+            edge_copy(t + LEAD).start()
+
+        consume(t, jnp.where(jnp.logical_or(t == 0, j == 0), 2, 0), CHUNK // SUB)
+
+        @pl.when(j == 0)
+        def _():
+            zp[0].start()
+
+        @pl.when(j == CHUNKS - 1)
+        def _():
+            zp[1].start()
+
+        whole = jnp.logical_and(t > 1, jnp.logical_and(j != 0, j != 1))
+
+        @pl.when(whole)
+        def _():
+            put(j - 1).start()
+
         return carry
 
-    lax.fori_loop(0, CHUNKS, consume_step, 0)
+    lax.fori_loop(0, CHUNKS - 1, step, 0)
+
+    consume(CHUNKS - 1, 0, CHUNK // SUB + 2)
+    put(FIRST - 2).start()
+    put(FIRST - 1).start()
+    put(FIRST).start()
 
     for c in zp:
         c.wait_recv()
@@ -415,23 +528,21 @@
     def _():
         parent[:, TOP + ROWS : TOP + ROWS + RIM, :] = jnp.zeros((4, RIM, BEAM), F32)
 
-    joint = FIRST * CHUNK
-    strips = (
-        (0, 0, RIM),
-        (joint - RIM, FIRST, 0),
-        (joint, FIRST, RIM),
-        (ROWS - RIM, CHUNKS, 0),
-    )
-    for n, (first, j, rho) in enumerate(strips):
-        range_two(first, n * SUB)
-    products(len(strips) * SUB)
-    for n, (first, j, rho) in enumerate(strips):
+    ends = ((0, 0, RIM), (ROWS - RIM, CHUNKS, 0))
+    for n, (first, j, rho) in enumerate(ends):
+        for e in range(2):
+            range_two(first, n * SUB, e, range_weights(e))
+    products(len(ends) * SUB)
+    for n, (first, j, rho) in enumerate(ends):
         finish(first, n * SUB, j, rho)
+    put(0).start()
+    put(CHUNKS - 1).start()
 
     for c in zc + zp:
         c.wait_send()
 
     def drain(t, carry):
+        put(t).wait()
         edge_copy(t).wait_send()
         for d in (1, 3, 2):
             window_copy(t, d).wait_send()
@@ -441,33 +552,38 @@
 
 
 def body(*args):
-    vmem = pl.BlockSpec(memory_space=pltpu.VMEM)
     dma = pltpu.SemaphoreType.DMA
     return pl.pallas_call(
         kernel,
         out_shape=jax.ShapeDtypeStruct((1, 2, ROWS, BEAM), F32),
-        in_specs=[pl.BlockSpec(memory_space=pl.ANY)] + [vmem] * 12,
-        out_specs=vmem,
-        scratch_shapes=[
+        in_specs=[pl.BlockSpec(memory_space=pl.ANY)] * 13,
+        out_specs=pl.BlockSpec(memory_space=pl.ANY),
+        scratch_shapes=[pltpu.VMEM(a.shape, a.dtype) for a in args[1:]]
+        + [
             pltpu.VMEM((2, ROWS + 2 * RIM, BEAM), F32),
             pltpu.VMEM((2, CHUNK, BEAM), F32),
             pltpu.VMEM((2, BEAM + 16, ROWS), F32),
             pltpu.VMEM((4, 2, WIN, ROWS), F32),
-            pltpu.VMEM((8, CHUNK, BEAM), F32),
+            pltpu.VMEM((8, NEAR, BEAM), F32),
             pltpu.VMEM((4, TOP + ROWS + 32, BEAM), F32),
-            pltpu.VMEM((4, CHUNK, 2 * BEAM), BF16),
+            pltpu.VMEM((4, NEAR, 2 * BEAM), BF16),
+            pltpu.VMEM((2, ROWS, BEAM), F32),
             pltpu.VMEM((OFFS, 8, BEAM), F32),
             pltpu.VMEM((2, OFFS, 8, BEAM), F32),
             pltpu.VMEM((2, 3 * WIN, BEAM), BF16),
             pltpu.VMEM((2, 2 * BEAM, BEAM), BF16),
             pltpu.VMEM((2, BEAM, BEAM), BF16),
-            pltpu.VMEM((4, CHUNK, BEAM), F32),
-            pltpu.VMEM((4, CHUNK, BEAM), F32),
-            pltpu.VMEM((4, 16, BEAM), F32),
-            pltpu.VMEM((4, 16, BEAM), F32),
-            pltpu.VMEM((32, BEAM), F32),
-            pltpu.VMEM((32, BEAM), F32),
+            pltpu.VMEM((4, NEAR, BEAM), F32),
+            pltpu.VMEM((4, NEAR, BEAM), F32),
+            pltpu.VMEM((4, FAR, BEAM), F32),
+            pltpu.VMEM((4, FAR, BEAM), F32),
+            pltpu.VMEM((24, BEAM), F32),
+            pltpu.VMEM((24, BEAM), F32),
             dma,
+            dma((CHUNKS,)),
+            dma((12,)),
+            pltpu.SemaphoreType.REGULAR,
+            pltpu.SemaphoreType.REGULAR,
             dma((2,)),
             dma((2,)),
             dma((2,)),
@@ -478,7 +594,7 @@
             dma((3, CHUNKS)),
         ],
         compiler_params=pltpu.CompilerParams(
-            collective_id=0, has_side_effects=True, vmem_limit_bytes=40 * 2**20
+            collective_id=0, has_side_effects=True, vmem_limit_bytes=60 * 2**20
         ),
         name="merge",
     )(*args)

time: 67.5 us -> 55.9 us (0.83)
  local copies, waits for them, and re-layouts: 11.5 us -> 3.05 us
  Pallas kernels: 55.3 us -> 52.6 us
    unnamed x27 -> x1, local copies, waits for them, and re-layouts: 11.5 us -> 3.05 us
    pallas_call x1, Pallas kernels: 55.3 us -> 52.6 us  [body(): pl.pallas_call(kernel, out_shape=jax.ShapeDtypeStruct((1, 2, ROWS, BEAM),...]
where the time goes in v1:
time: 55.9 us; the launch traced here: 55.7 us
  Pallas kernels  52.6 us (94%)
  local copies, waits for them, and re-layouts  3.05 us (5%)
    pallas_call x1, Pallas kernels, body(): pl.pallas_call(kernel, out_shape=jax.ShapeDtypeStruct((1, 2, ROWS, BEAM),...  52.6 us
    unnamed x1, local copies, waits for them, and re-layouts  3.05 us

profile of v1, /device:TPU:1, one launch (start us, length us, event | category | flops | bytes accessed | tf_op | source)
XLA Modules:
  0.0 55.7 jit_solution(17333885422124637412)
XLA Ops:
  0.0 52.6 %merge.1 = f32[1,2,2048,128]{3,2,1,0:T(8,128)} custom-call(f32[1,2,2048,128]{3,2,1,0:T(8,128)} %child_hbm.1, s32[2,256]{1,0:T(2,128)} %sh1_hbm.1, f32[2,8,256]{2,1,0:T(8,128)} %rt1_hbm.1, s32[2,512]{1,0:T(2,128)} %bs1_hbm.1, f32[2,8,512]{2,1,0:T(8,128)} %bt1_hbm.1, f32[2,512]{1,0:T(2,128)} %pr1_hbm.1, f32[2,512]{1,0:T(2,128)} %po1_hbm.1, s32[2,512]{1,0:T(2,128)} %sh2_hbm.1, ...), custom_call_target="tpu_custom_call" | custom-call | tf_op jit(solution)/shard_map/merge/pallas_call | solution.py:556
  52.6 3.0 %copy.15 = f32[1,2,2048,128]{3,2,1,0:T(8,128)} copy(f32[1,2,2048,128]{3,2,1,0:T(8,128)} %merge.1) | data formatting | bytes 4194304

commit v2 on v1

--- a/solution.py
+++ b/solution.py
@@ -13,13 +13,14 @@
 CHUNK = 128
 CHUNKS = ROWS // CHUNK
 FIRST = 7
-EARLY = 3
+EARLY = 1
 LEAD = 6
 NEAR = CHUNK + 32
 FAR = 24
 WIN = 48
 TAPS = 8
-OFFS = 24
+FINE = 12
+COARSE = 4
 RIM = 16
 TOP = 32
 SUB = 16
@@ -33,12 +34,41 @@
     return hi, lo
 
 
-def range_table(shift_row, tap_rows, out_ref):
-    for o in range(OFFS):
+def range_table(shift_row, tap_rows, out_ref, step_ref):
+    shift = shift_row + 8
+    q = jnp.minimum(lax.shift_right_logical(shift, 2), COARSE - 1)
+    p = shift - 4 * q
+    step_ref[...] = jnp.broadcast_to(q, (8, BEAM))
+    for o in range(FINE):
         acc = jnp.zeros((1, BEAM), F32)
         for k in range(TAPS):
-            acc = acc + jnp.where(shift_row + (8 + k) == o, tap_rows[k : k + 1], 0.0)
+            acc = acc + jnp.where(p + k == o, tap_rows[k : k + 1], 0.0)
         out_ref[o] = jnp.broadcast_to(acc, (8, BEAM))
+
+
+def fine_rows(src, comps, first, weights, dst, slot):
+    for n, comp in enumerate(comps):
+        for v in range(2):
+            acc = None
+            for o in range(FINE):
+                term = weights[o] * src[comp, pl.ds(first + (o + 8 * v), 8), :]
+                acc = term if acc is None else acc + term
+            dst[n, pl.ds(pl.multiple_of(slot + 8 * v, 8), 8), :] = acc
+
+
+def coarse_rows(src, comp, slot, picks):
+    out = []
+    for v in range(2):
+        rows = [src[comp, pl.ds(slot + (4 * q + 8 * v), 8), :] for q in range(COARSE)]
+        low = jnp.where(picks[0], rows[0], rows[1])
+        high = jnp.where(picks[2], rows[2], rows[3])
+        out.append(jnp.where(picks[1], low, high))
+    return out
+
+
+def picks_of(step_ref):
+    q = step_ref[...]
+    return [q == 0, q < 2, q == 2]
 
 
 def beam_matrix(rows, start_row, tap_rows):
@@ -111,6 +141,9 @@
     image,
     tab1,
     tab2,
+    step1,
+    step2,
+    fine,
     mat1,
     mat2a,
     mat2b,
@@ -148,7 +181,15 @@
     def chunk_of(t):
         return lax.rem(t + FIRST, CHUNKS)
 
-    load = pltpu.make_async_copy(child_hbm.at[0], child.at[:, pl.ds(RIM, ROWS), :], in_sem)
+    cut = (0, FIRST * CHUNK - RIM, (FIRST + EARLY) * CHUNK + RIM, ROWS)
+    loads = [
+        pltpu.make_async_copy(
+            child_hbm.at[0, :, pl.ds(cut[n], cut[n + 1] - cut[n]), :],
+            child.at[:, pl.ds(RIM + cut[n], cut[n + 1] - cut[n]), :],
+            in_sem.at[n],
+        )
+        for n in (1, 2, 0)
+    ]
     tables = [
         pltpu.make_async_copy(src, dst, tab_sem.at[n])
         for n, (src, dst) in enumerate(
@@ -170,7 +211,8 @@
     ]
     for c in tables[:2]:
         c.start()
-    load.start()
+    for c in loads:
+        c.start()
     for c in tables[2:]:
         c.start()
 
@@ -187,6 +229,14 @@
     @pl.when(beam == 1)
     def _():
         pl.semaphore_signal(barrier, inc=1, device_id=partner, device_id_type=MESH)
+
+    @pl.when(beam == 0)
+    def _():
+        pl.semaphore_wait(barrier, 4)
+        for d in (1, 2, 3):
+            pl.semaphore_signal(
+                chip_sem, inc=1, device_id=(group + peer(d), rng, beam), device_id_type=MESH
+            )
 
     @pl.when(beam == 0)
     def _():
@@ -201,7 +251,7 @@
     side = lax.div(me, 2)
     own = pl.ds(pl.multiple_of(beam * BEAM, BEAM), BEAM)
     shift_row = jnp.where(side == 0, sh1[0:1, own], sh1[1:2, own])
-    range_table(shift_row, rt1[side, :, own], tab1)
+    range_table(shift_row, rt1[side, :, own], tab1, step1)
 
     def halo(buf, sem_s, sem_r, first, last, low, high):
         return (
@@ -253,43 +303,56 @@
         j = chunk_of(t)
         base = pl.multiple_of(j * CHUNK, CHUNK)
 
-        def rows(s, carry):
-            first = base + s * 32
+        weights = [tab1[o] for o in range(FINE)]
+        picks = picks_of(step1)
+
+        def fine_in(s, carry):
+            slot = pl.multiple_of(s * SUB, SUB)
+            fine_rows(child, (0, 1), base + (RIM - 16) + slot, weights, fine, slot)
+            return carry
+
+        def coarse_in(s, carry):
+            slot = pl.multiple_of(s * SUB, SUB)
             for comp in range(2):
-                acc = [jnp.zeros((8, BEAM), F32) for _ in range(4)]
-                for o in range(OFFS):
-                    w = tab1[o]
-                    for v in range(4):
-                        acc[v] = acc[v] + w * child[comp, pl.ds(first + (o + 4 + 8 * v), 8), :]
-                for v in range(4):
-                    wide[comp, pl.ds(pl.multiple_of(s * 32 + 8 * v, 8), 8), :] = acc[v]
+                for v, x in enumerate(coarse_rows(fine, comp, slot + 4, picks)):
+                    wide[comp, pl.ds(pl.multiple_of(slot + 8 * v, 8), 8), :] = x
             return carry
 
-        lax.fori_loop(0, CHUNK // 32, rows, 0)
+        lax.fori_loop(0, CHUNK // SUB + 1, fine_in, 0)
+        lax.fori_loop(0, CHUNK // SUB, coarse_in, 0)
         for comp in range(2):
             for half in range(CHUNK // BEAM):
                 turned[
                     comp, 8:136, pl.ds(pl.multiple_of(base + half * BEAM, BEAM), BEAM)
                 ] = jnp.transpose(wide[comp, half * BEAM : (half + 1) * BEAM, :])
 
+    def inner(d):
+        return jnp.logical_or(peer(d) == 1, peer(d) == 2)
+
     def send(t):
         edge_copy(t).wait_recv()
         for d in (1, 3, 2):
             window_copy(t, d).start()
+        keep(t)
+
+    def keep(t):
         at = pl.ds(pl.multiple_of(chunk_of(t) * CHUNK, CHUNK), CHUNK)
         got[me, :, :, at] = turned[:, pl.ds(pl.multiple_of(32 * me, 8), WIN), at]
 
-    load.wait()
-    for t in range(EARLY):
-        produce(t)
+    loads[0].wait()
+    produce(0)
+
+    def open_windows():
+        edge_copy(0).start()
+        for d in (1, 3, 2):
+
+            @pl.when(inner(d))
+            def _(d=d):
+                window_copy(0, d).start()
 
     @pl.when(beam == 0)
     def _():
-        pl.semaphore_wait(barrier, 4)
-        for d in (1, 2, 3):
-            pl.semaphore_signal(
-                chip_sem, inc=1, device_id=(group + peer(d), rng, beam), device_id_type=MESH
-            )
+        open_windows()
         pl.semaphore_wait(chip_sem, 3)
         pl.semaphore_signal(core_sem, inc=1, device_id=partner, device_id_type=MESH)
 
@@ -298,17 +361,40 @@
         pl.semaphore_wait(core_sem, 1)
         for z in (up, down):
             pl.semaphore_signal(barrier, inc=1, device_id=(aper, z, beam), device_id_type=MESH)
-
-    for t in range(EARLY):
-        edge_copy(t).start()
-    for t in range(EARLY, LEAD):
+        open_windows()
+
+    loads[1].wait()
+    produce(1)
+    edge_copy(1).start()
+    edge_copy(0).wait_recv()
+    for d in (1, 3, 2):
+
+        @pl.when(jnp.logical_not(inner(d)))
+        def _(d=d):
+            window_copy(0, d).start()
+
+    keep(0)
+    loads[2].wait()
+
+    def lead_step(t, carry):
         produce(t)
         edge_copy(t).start()
-        if t == EARLY:
-            for before in range(EARLY):
-                send(before)
-        else:
-            send(t - 1)
+        send(t - 1)
+        return carry
+
+    lax.fori_loop(2, LEAD, lead_step, 0)
+
+    @pl.when(beam == 1)
+    def _():
+        pl.semaphore_wait(barrier, 2)
+        pl.semaphore_signal(core_sem, inc=1, device_id=partner, device_id_type=MESH)
+
+    @pl.when(beam == 0)
+    def _():
+        pl.semaphore_wait(core_sem, 1)
+
+    for c in zc:
+        c.start()
 
     for c in tables[2:]:
         c.wait()
@@ -329,7 +415,7 @@
         mat1[s, 0:WIN, :] = hi
         mat1[s, WIN : 2 * WIN, :] = hi
         mat1[s, 2 * WIN : 3 * WIN, :] = lo
-        range_table(ints[2 + s : 3 + s], lanes(rt2[s]), tab2.at[s])
+        range_table(ints[2 + s : 3 + s], lanes(rt2[s]), tab2.at[s], step2.at[s])
         m = beam_matrix(BEAM, bs2[s : s + 1, final] - (64 * block - 8), bt2[s, :, final])
         hi, lo = split_bf16(m)
         mat2a[s, 0:BEAM, :] = hi
@@ -360,18 +446,6 @@
             tmp_s,
         )
 
-    @pl.when(beam == 1)
-    def _():
-        pl.semaphore_wait(barrier, 2)
-        pl.semaphore_signal(core_sem, inc=1, device_id=partner, device_id_type=MESH)
-
-    @pl.when(beam == 0)
-    def _():
-        pl.semaphore_wait(core_sem, 1)
-
-    for c in zc:
-        c.start()
-
     def turn(level, j, rho):
         both = []
         for s in range(2):
@@ -385,14 +459,14 @@
     def make_parents(j):
         at = pl.ds(pl.multiple_of(j * CHUNK, CHUNK), CHUNK)
         for c in range(4):
-            for comp in range(2):
-                hi, lo = split_bf16(got[c, comp, :, at])
-                mixed[2 * c + comp, 0:CHUNK, :] = lax.dot_general(
-                    jnp.concatenate([hi, lo, hi], axis=0),
-                    mat1[c // 2],
-                    (((0,), (0,)), ((), ())),
-                    preferred_element_type=F32,
-                )
+            both = jnp.concatenate([got[c, 0, :, at], got[c, 1, :, at]], axis=1)
+            hi, lo = split_bf16(both)
+            mixed[2 * c : 2 * c + 2, 0:CHUNK, :] = lax.dot_general(
+                jnp.concatenate([hi, lo, hi], axis=0),
+                mat1[c // 2],
+                (((0,), (0,)), ((), ())),
+                preferred_element_type=F32,
+            ).reshape(2, CHUNK, BEAM)
 
         def rows(s, carry):
             rho = pl.multiple_of(s * SUB, SUB)
@@ -408,29 +482,28 @@
 
         lax.fori_loop(0, CHUNK // SUB, rows, 0)
 
-    def range_two(first, slot, e, weights):
-        acc = [[jnp.zeros((8, BEAM), F32) for _ in range(2)] for _ in range(2)]
-        for o in range(OFFS):
-            for comp in range(2):
-                for v in range(2):
-                    acc[comp][v] = acc[comp][v] + weights[o] * parent[
-                        2 * e + comp, pl.ds(first + (TOP - 12 + o + 8 * v), 8), :
-                    ]
+    def fine_two(first, slot, e, weights):
+        fine_rows(
+            parent, (2 * e, 2 * e + 1), first + TOP, weights, fine.at[pl.ds(2 * e, 2)], slot
+        )
+
+    def coarse_two(slot, from_slot, e, picks):
         for comp in range(2):
-            hi, lo = split_bf16(jnp.concatenate(acc[comp], axis=0))
+            rows = coarse_rows(fine, 2 * e + comp, from_slot + 4, picks)
+            hi, lo = split_bf16(jnp.concatenate(rows, axis=0))
             packed[2 * e + comp, pl.ds(slot, SUB), 0:BEAM] = hi
             packed[2 * e + comp, pl.ds(slot, SUB), BEAM : 2 * BEAM] = lo
 
-    def range_weights(e):
-        return [tab2[e, o] for o in range(OFFS)]
+    def weights_two(e):
+        return [tab2[e, o] for o in range(FINE)]
 
     def products(count):
         for e in range(2):
-            for comp in range(2):
-                z = packed[2 * e + comp, 0:count, :]
-                mixed[2 * e + comp, 0:count, :] = jnp.dot(
-                    z, mat2a[e], preferred_element_type=F32
-                ) + jnp.dot(z[:, :BEAM], mat2b[e], preferred_element_type=F32)
+            z = packed[2 * e : 2 * e + 2, 0:count, :].reshape(2 * count, 2 * BEAM)
+            mixed[2 * e : 2 * e + 2, 0:count, :] = (
+                jnp.dot(z, mat2a[e], preferred_element_type=F32)
+                + jnp.dot(z[:, :BEAM], mat2b[e], preferred_element_type=F32)
+            ).reshape(2, count, BEAM)
 
     def finish(first, slot, j, rho):
         (c0, s0), (c1, s1) = turn(1, j, rho)
@@ -450,9 +523,14 @@
             window_copy(t, d).wait_recv()
         make_parents(j)
 
-        def rows_in(s, carry, e, weights):
+        def fine_in(s, carry, e, weights):
             slot = pl.multiple_of(s * SUB, SUB)
-            range_two(pl.multiple_of(j * CHUNK - RIM + slot, SUB), slot, e, weights)
+            fine_two(j * CHUNK - 2 * RIM + slot, slot, e, weights)
+            return carry
+
+        def coarse_in(s, carry, e, picks):
+            slot = pl.multiple_of(s * SUB, SUB)
+            coarse_two(slot, slot, e, picks)
             return carry
 
         def rows_out(s, carry):
@@ -462,7 +540,10 @@
 
         for e in range(2):
             lax.fori_loop(
-                begin, end, functools.partial(rows_in, e=e, weights=range_weights(e)), 0
+                begin, end + 1, functools.partial(fine_in, e=e, weights=weights_two(e)), 0
+            )
+            lax.fori_loop(
+                begin, end, functools.partial(coarse_in, e=e, picks=picks_of(step2.at[e])), 0
             )
         products(end * SUB)
         lax.fori_loop(begin, end, rows_out, 0)
@@ -512,31 +593,33 @@
 
     lax.fori_loop(0, CHUNKS - 1, step, 0)
 
+    for c in zp:
+        c.wait_recv()
+
+    @pl.when(rng == 0)
+    def _():
+        parent[:, TOP - RIM : TOP, :] = jnp.zeros((4, RIM, BEAM), F32)
+
+    @pl.when(rng == 3)
+    def _():
+        parent[:, TOP + ROWS : TOP + ROWS + RIM, :] = jnp.zeros((4, RIM, BEAM), F32)
+
+    ends = ((0, 0, RIM), (ROWS - RIM, CHUNKS, 0))
+    for n, (first, j, rho) in enumerate(ends):
+        for e in range(2):
+            for half in range(2):
+                fine_two(first - RIM + half * SUB, half * SUB, e, weights_two(e))
+            coarse_two(n * SUB, 0, e, picks_of(step2.at[e]))
+    products(len(ends) * SUB)
+    for n, (first, j, rho) in enumerate(ends):
+        finish(first, n * SUB, j, rho)
+
+    put(0).start()
+    put(CHUNKS - 1).start()
     consume(CHUNKS - 1, 0, CHUNK // SUB + 2)
     put(FIRST - 2).start()
     put(FIRST - 1).start()
     put(FIRST).start()
-
-    for c in zp:
-        c.wait_recv()
-
-    @pl.when(rng == 0)
-    def _():
-        parent[:, TOP - RIM : TOP, :] = jnp.zeros((4, RIM, BEAM), F32)
-
-    @pl.when(rng == 3)
-    def _():
-        parent[:, TOP + ROWS : TOP + ROWS + RIM, :] = jnp.zeros((4, RIM, BEAM), F32)
-
-    ends = ((0, 0, RIM), (ROWS - RIM, CHUNKS, 0))
-    for n, (first, j, rho) in enumerate(ends):
-        for e in range(2):
-            range_two(first, n * SUB, e, range_weights(e))
-    products(len(ends) * SUB)
-    for n, (first, j, rho) in enumerate(ends):
-        finish(first, n * SUB, j, rho)
-    put(0).start()
-    put(CHUNKS - 1).start()
 
     for c in zc + zp:
         c.wait_send()
@@ -568,8 +651,11 @@
             pltpu.VMEM((4, TOP + ROWS + 32, BEAM), F32),
             pltpu.VMEM((4, NEAR, 2 * BEAM), BF16),
             pltpu.VMEM((2, ROWS, BEAM), F32),
-            pltpu.VMEM((OFFS, 8, BEAM), F32),
-            pltpu.VMEM((2, OFFS, 8, BEAM), F32),
+            pltpu.VMEM((FINE, 8, BEAM), F32),
+            pltpu.VMEM((2, FINE, 8, BEAM), F32),
+            pltpu.VMEM((8, BEAM), jnp.int32),
+            pltpu.VMEM((2, 8, BEAM), jnp.int32),
+            pltpu.VMEM((4, NEAR + SUB, BEAM), F32),
             pltpu.VMEM((2, 3 * WIN, BEAM), BF16),
             pltpu.VMEM((2, 2 * BEAM, BEAM), BF16),
             pltpu.VMEM((2, BEAM, BEAM), BF16),
@@ -579,7 +665,7 @@
             pltpu.VMEM((4, FAR, BEAM), F32),
             pltpu.VMEM((24, BEAM), F32),
             pltpu.VMEM((24, BEAM), F32),
-            dma,
+            dma((3,)),
             dma((CHUNKS,)),
             dma((12,)),
             pltpu.SemaphoreType.REGULAR,

time: 55.9 us -> 53.4 us (0.955)
  Pallas kernels: 52.6 us -> 50.2 us
    pallas_call x1, Pallas kernels: 52.6 us -> 50.2 us  [body(): pl.pallas_call(kernel, out_shape=jax.ShapeDtypeStruct((1, 2, ROWS, BEAM),...]
where the time goes in v2:
time: 53.4 us; the launch traced here: 53.2 us
  Pallas kernels  50.2 us (94%)
  local copies, waits for them, and re-layouts  3.05 us (6%)
    pallas_call x1, Pallas kernels, body(): pl.pallas_call(kernel, out_shape=jax.ShapeDtypeStruct((1, 2, ROWS, BEAM),...  50.2 us
    unnamed x1, local copies, waits for them, and re-layouts  3.05 us

profile of v2, /device:TPU:1, one launch (start us, length us, event | category | flops | bytes accessed | tf_op | source)
XLA Modules:
  0.0 53.2 jit_solution(6410093441997742795)
XLA Ops:
  0.0 50.2 %merge.1 = f32[1,2,2048,128]{3,2,1,0:T(8,128)} custom-call(f32[1,2,2048,128]{3,2,1,0:T(8,128)} %child_hbm.1, s32[2,256]{1,0:T(2,128)} %sh1_hbm.1, f32[2,8,256]{2,1,0:T(8,128)} %rt1_hbm.1, s32[2,512]{1,0:T(2,128)} %bs1_hbm.1, f32[2,8,512]{2,1,0:T(8,128)} %bt1_hbm.1, f32[2,512]{1,0:T(2,128)} %pr1_hbm.1, f32[2,512]{1,0:T(2,128)} %po1_hbm.1, s32[2,512]{1,0:T(2,128)} %sh2_hbm.1, ...), custom_call_target="tpu_custom_call" | custom-call | tf_op jit(solution)/shard_map/merge/pallas_call | solution.py:639
  50.2 3.0 %copy.15 = f32[1,2,2048,128]{3,2,1,0:T(8,128)} copy(f32[1,2,2048,128]{3,2,1,0:T(8,128)} %merge.1) | data formatting | bytes 4194304

commit v3 on v2

--- a/solution.py
+++ b/solution.py
@@ -118,7 +118,7 @@
     bt2_hbm,
     pr2_hbm,
     po2_hbm,
-    out,
+    image,
     sh1,
     rt1,
     bs1,
@@ -138,7 +138,6 @@
     mixed,
     parent,
     packed,
-    image,
     tab1,
     tab2,
     step1,
@@ -154,7 +153,6 @@
     tmp_c,
     tmp_s,
     in_sem,
-    out_sem,
     tab_sem,
     chip_sem,
     core_sem,
@@ -510,12 +508,8 @@
         here = pl.ds(slot, SUB)
         to = pl.ds(first, SUB)
         lr, li, rr, ri = (mixed[i, here, :] for i in range(4))
-        image[0, to, :] = (c0 * lr - s0 * li) + (c1 * rr - s1 * ri)
-        image[1, to, :] = (s0 * lr + c0 * li) + (s1 * rr + c1 * ri)
-
-    def put(j):
-        at = pl.ds(pl.multiple_of(j * CHUNK, CHUNK), CHUNK)
-        return pltpu.make_async_copy(image.at[:, at, :], out.at[0, :, at, :], out_sem.at[j])
+        image[0, 0, to, :] = (c0 * lr - s0 * li) + (c1 * rr - s1 * ri)
+        image[0, 1, to, :] = (s0 * lr + c0 * li) + (s1 * rr + c1 * ri)
 
     def consume(t, begin, end):
         j = chunk_of(t)
@@ -583,12 +577,6 @@
         def _():
             zp[1].start()
 
-        whole = jnp.logical_and(t > 1, jnp.logical_and(j != 0, j != 1))
-
-        @pl.when(whole)
-        def _():
-            put(j - 1).start()
-
         return carry
 
     lax.fori_loop(0, CHUNKS - 1, step, 0)
@@ -614,18 +602,12 @@
     for n, (first, j, rho) in enumerate(ends):
         finish(first, n * SUB, j, rho)
 
-    put(0).start()
-    put(CHUNKS - 1).start()
     consume(CHUNKS - 1, 0, CHUNK // SUB + 2)
-    put(FIRST - 2).start()
-    put(FIRST - 1).start()
-    put(FIRST).start()
 
     for c in zc + zp:
         c.wait_send()
 
     def drain(t, carry):
-        put(t).wait()
         edge_copy(t).wait_send()
         for d in (1, 3, 2):
             window_copy(t, d).wait_send()
@@ -636,11 +618,12 @@
 
 def body(*args):
     dma = pltpu.SemaphoreType.DMA
+    args = [pltpu.with_memory_space_constraint(a, pltpu.HBM) for a in args]
     return pl.pallas_call(
         kernel,
         out_shape=jax.ShapeDtypeStruct((1, 2, ROWS, BEAM), F32),
         in_specs=[pl.BlockSpec(memory_space=pl.ANY)] * 13,
-        out_specs=pl.BlockSpec(memory_space=pl.ANY),
+        out_specs=pl.BlockSpec(memory_space=pltpu.VMEM),
         scratch_shapes=[pltpu.VMEM(a.shape, a.dtype) for a in args[1:]]
         + [
             pltpu.VMEM((2, ROWS + 2 * RIM, BEAM), F32),
@@ -650,7 +633,6 @@
             pltpu.VMEM((8, NEAR, BEAM), F32),
             pltpu.VMEM((4, TOP + ROWS + 32, BEAM), F32),
             pltpu.VMEM((4, NEAR, 2 * BEAM), BF16),
-            pltpu.VMEM((2, ROWS, BEAM), F32),
             pltpu.VMEM((FINE, 8, BEAM), F32),
             pltpu.VMEM((2, FINE, 8, BEAM), F32),
             pltpu.VMEM((8, BEAM), jnp.int32),
@@ -666,7 +648,6 @@
             pltpu.VMEM((24, BEAM), F32),
             pltpu.VMEM((24, BEAM), F32),
             dma((3,)),
-            dma((CHUNKS,)),
             dma((12,)),
             pltpu.SemaphoreType.REGULAR,
             pltpu.SemaphoreType.REGULAR,
@@ -680,7 +661,7 @@
             dma((3, CHUNKS)),
         ],
         compiler_params=pltpu.CompilerParams(
-            collective_id=0, has_side_effects=True, vmem_limit_bytes=60 * 2**20
+            collective_id=0, has_side_effects=True, vmem_limit_bytes=36 * 2**20
         ),
         name="merge",
     )(*args)

time: 53.4 us -> 50.8 us (0.951)
  local copies, waits for them, and re-layouts: 3.05 us -> 1.32 us
  Pallas kernels: 50.2 us -> 49.3 us
    unnamed x1, local copies, waits for them, and re-layouts: 3.05 us -> 1.32 us
    pallas_call x1, Pallas kernels: 50.2 us -> 49.3 us  [body(): pl.pallas_call(kernel, out_shape=jax.ShapeDtypeStruct((1, 2, ROWS, BEAM),...]
where the time goes in v3:
time: 50.8 us; the launch traced here: 50.7 us
  Pallas kernels  49.3 us (97%)
  local copies, waits for them, and re-layouts  1.32 us (3%)
    pallas_call x1, Pallas kernels, body(): pl.pallas_call(kernel, out_shape=jax.ShapeDtypeStruct((1, 2, ROWS, BEAM),...  49.3 us
    unnamed x1, local copies, waits for them, and re-layouts  1.32 us

profile of v3, /device:TPU:1, one launch (start us, length us, event | category | flops | bytes accessed | tf_op | source)
XLA Modules:
  0.0 50.7 jit_solution(14198242054758320424)
XLA Ops:
  0.0 49.3 %merge.1 = f32[1,2,2048,128]{3,2,1,0:T(8,128)S(1)} custom-call(f32[1,2,2048,128]{3,2,1,0:T(8,128)} %child_hbm.1, s32[2,256]{1,0:T(2,128)} %sh1_hbm.1, f32[2,8,256]{2,1,0:T(8,128)} %rt1_hbm.1, s32[2,512]{1,0:T(2,128)} %bs1_hbm.1, f32[2,8,512]{2,1,0:T(8,128)} %bt1_hbm.1, f32[2,512]{1,0:T(2,128)} %pr1_hbm.1, f32[2,512]{1,0:T(2,128)} %po1_hbm.1, ...), custom_call_target="tpu_custom_call" | custom-call | tf_op jit(solution)/shard_map/merge/pallas_call | solution.py:622
  49.3 1.3 %copy.15 = f32[1,2,2048,128]{3,2,1,0:T(8,128)} copy(f32[1,2,2048,128]{3,2,1,0:T(8,128)S(1)} %merge.1) | data formatting | bytes 4194304

commit v4 on v3

--- a/solution.py
+++ b/solution.py
@@ -329,7 +329,7 @@
 
     def send(t):
         edge_copy(t).wait_recv()
-        for d in (1, 3, 2):
+        for d in (2, 1, 3):
             window_copy(t, d).start()
         keep(t)
 
@@ -342,7 +342,7 @@
 
     def open_windows():
         edge_copy(0).start()
-        for d in (1, 3, 2):
+        for d in (2, 1, 3):
 
             @pl.when(inner(d))
             def _(d=d):
@@ -365,7 +365,7 @@
     produce(1)
     edge_copy(1).start()
     edge_copy(0).wait_recv()
-    for d in (1, 3, 2):
+    for d in (2, 1, 3):
 
         @pl.when(jnp.logical_not(inner(d)))
         def _(d=d):
@@ -513,7 +513,7 @@
 
     def consume(t, begin, end):
         j = chunk_of(t)
-        for d in (1, 3, 2):
+        for d in (2, 1, 3):
             window_copy(t, d).wait_recv()
         make_parents(j)
 
@@ -609,7 +609,7 @@
 
     def drain(t, carry):
         edge_copy(t).wait_send()
-        for d in (1, 3, 2):
+        for d in (2, 1, 3):
             window_copy(t, d).wait_send()
         return carry
 

time: 50.8 us -> 51.7 us (1.018)
  Pallas kernels: 49.3 us -> 50.2 us
    pallas_call x1, Pallas kernels: 49.3 us -> 50.2 us  [body(): pl.pallas_call(kernel, out_shape=jax.ShapeDtypeStruct((1, 2, ROWS, BEAM),...]
where the time goes in v4:
time: 51.7 us; the launch traced here: 51.5 us
  Pallas kernels  50.2 us (97%)
  local copies, waits for them, and re-layouts  1.32 us (3%)
    pallas_call x1, Pallas kernels, body(): pl.pallas_call(kernel, out_shape=jax.ShapeDtypeStruct((1, 2, ROWS, BEAM),...  50.2 us
    unnamed x1, local copies, waits for them, and re-layouts  1.32 us

profile of v4, /device:TPU:1, one launch (start us, length us, event | category | flops | bytes accessed | tf_op | source)
XLA Modules:
  0.0 51.5 jit_solution(5631206658964496739)
XLA Ops:
  0.0 50.2 %merge.1 = f32[1,2,2048,128]{3,2,1,0:T(8,128)S(1)} custom-call(f32[1,2,2048,128]{3,2,1,0:T(8,128)} %child_hbm.1, s32[2,256]{1,0:T(2,128)} %sh1_hbm.1, f32[2,8,256]{2,1,0:T(8,128)} %rt1_hbm.1, s32[2,512]{1,0:T(2,128)} %bs1_hbm.1, f32[2,8,512]{2,1,0:T(8,128)} %bt1_hbm.1, f32[2,512]{1,0:T(2,128)} %pr1_hbm.1, f32[2,512]{1,0:T(2,128)} %po1_hbm.1, ...), custom_call_target="tpu_custom_call" | custom-call | tf_op jit(solution)/shard_map/merge/pallas_call | solution.py:622
  50.2 1.3 %copy.15 = f32[1,2,2048,128]{3,2,1,0:T(8,128)} copy(f32[1,2,2048,128]{3,2,1,0:T(8,128)S(1)} %merge.1) | data formatting | bytes 4194304
